TPU v7x, 32 devices: a whole 2x2x4 slice. The times are simulated.
32 devices in a mesh: groups: 2 (over y), frame: 4 (over z), space: 2 (over x), head: 2 (over core).
Axes of the slice: x: 2, y: 2, z: 4, core: 2. Of those that a mesh axis runs over, the one named last changes fastest.
Arguments:
- queries: bfloat16 [8, 512, 3072], P(('groups', 'frame'), 'space', 'head'), parts along dimension 0, may hold values from -6 to 6
- key_states: bfloat16 [8, 512, 3072], P(('groups', 'frame'), 'space', 'head'), parts along dimension 0, may hold values from -24 to 24
- value_states: bfloat16 [8, 512, 3072], P(('groups', 'frame'), 'space', 'head'), parts along dimension 0, may hold values from -6 to 6
- profile: int32 [24], replicated, may hold values from 0 to 1, as said below
- window: int32 [24], replicated, may hold values from 1 to 4, as said below
Outputs:
- attended: bfloat16 [8, 512, 3072], P(('groups', 'frame'), 'space', 'head'), parts along dimension 0
There are 2 independent parts, one for each index of `groups`. A program takes and returns all parts, laid end to end along the dimension named above; an argument that names none is the same for every part. Nothing has to cross between parts.
Inputs may be any that keep to these rules, and one draw needn't show every extreme that they name: `profile`: 1 marks a head of frame-local attention, 0 a head of attention over a window of frames; exactly half of the 24 heads are marked 1. Some head marked 0 in profile has window 4.
All inputs are finite; a program needn't handle non-finite values.
Results may differ from a plain program's by a relative error of at most 0.0055.
Values may be sent and summed in bfloat16 or wider, within the bound.
A program may use at most 64 MiB of HBM per device.

v0:
```python
import functools

import jax
import jax.numpy as jnp
from jax import lax
from jax.experimental import pallas as pl
from jax.experimental.pallas import tpu as pltpu
from jax.sharding import PartitionSpec as P

HD = 128
WMAX = 4
MESH = pl.DeviceIdType.MESH


def kernel(
    frames, spaces, cores, prof_hbm, win_hbm, q_ref, k_ref, v_ref, out_ref,
    full, mine_first, theirs, squery, kv, tsend, trecv, tout, res,
    prof_ref, win_ref, pos, place, order, tab,
    loc_sem, d_send, d_recv, s_send, s_recv, t_send, t_recv, o_send, o_recv, r_send, r_recv,
):
    rows = q_ref.shape[1]
    here = q_ref.shape[2] // HD
    share = here // 2
    part = rows // frames
    scale = HD ** (-0.5)
    f = lax.axis_index("frame")
    x = lax.axis_index("space")
    c = lax.axis_index("head")
    others_f = [lax.rem(f + d, frames) for d in range(1, frames)]
    others_x = [lax.rem(x + d, spaces) for d in range(1, spaces)]
    others_c = [lax.rem(c + d, cores) for d in range(1, cores)]
    side = f // (frames // 2)
    far_first = [
        lax.rem(f + (1 - side) * (frames - 1 - i) + side * (1 + i), frames)
        for i in range(frames - 1)
    ]

    def remote(src, dst, send, recv, **target):
        return pltpu.make_async_remote_copy(
            src_ref=src, dst_ref=dst, send_sem=send, recv_sem=recv,
            device_id=target, device_id_type=MESH,
        )

    def lanes(h):
        return pl.ds(pl.multiple_of(h * HD, HD), HD)

    small = (
        pltpu.make_async_copy(prof_hbm, prof_ref, loc_sem.at[3]),
        pltpu.make_async_copy(win_hbm, win_ref, loc_sem.at[4]),
    )
    for copy in small:
        copy.start()
    sources = (k_ref, v_ref, q_ref)
    for n, src in enumerate(sources):
        def local_start(h, _):
            pltpu.make_async_copy(src.at[0, :, lanes(h)], full.at[n, h], loc_sem.at[n]).start()
            return 0

        lax.fori_loop(0, here, local_start, 0)

    barrier = pltpu.get_barrier_semaphore()
    for other in others_c:
        pl.semaphore_signal(barrier, inc=1, device_id={"head": other}, device_id_type=MESH)
    for other in others_x:
        pl.semaphore_signal(barrier, inc=1, device_id={"space": other}, device_id_type=MESH)
    for other in others_f:
        pl.semaphore_signal(barrier, inc=1, device_id={"frame": other}, device_id_type=MESH)

    for copy in small:
        copy.wait()

    count = jnp.int32(0)
    for h in range(here):
        count = count + prof_ref[h]
    first_space = (count >= share).astype(jnp.int32)
    main_count = jnp.maximum(count, here - count)
    for e in range(cores):
        main = first_space if e == 0 else 1 - first_space
        major = jnp.int32(0)
        minor = main_count
        for h in range(here):
            p = prof_ref[e * here + h]
            is_main = p * main + (1 - p) * (1 - main)
            slot = jnp.clip(is_main * major + (1 - is_main) * minor, 0, here - 1)
            major = major + is_main
            minor = minor + (1 - is_main)
            away = ((slot >= share) & (slot < main_count)).astype(jnp.int32)
            owner = away * (1 - e) + (1 - away) * e
            pos[e * here + h] = slot
            place[e * here + h] = owner * here + (1 - p) * share + slot - (slot >= share).astype(jnp.int32) * share

    def fill(slot, _):
        head = jnp.int32(0)
        for h in range(here):
            head = head + jnp.where(pos[c * here + h] == slot, h, 0)
        order[slot] = jnp.clip(head, 0, here - 1)
        return 0

    lax.fori_loop(0, here, fill, 0)

    for n in range(3):
        pltpu.make_async_copy(full.at[n], full.at[n], loc_sem.at[n]).wait()

    def arrange(slot, _):
        head = order[slot]
        for n in range(3):
            mine_first[slot, n] = full[n, head]
        return 0

    lax.fori_loop(0, here, arrange, 0)

    pl.semaphore_wait(barrier, len(others_c) + len(others_x) + len(others_f))

    partner = others_c[0]

    def core_copy(j):
        return remote(mine_first.at[share + j], theirs.at[j], d_send.at[j], d_recv.at[j], head=partner)

    def core_start(j, _):
        core_copy(j).start()
        return 0

    lax.fori_loop(0, share, core_start, 0)

    main_space = c * (1 - first_space) + (1 - c) * first_space
    my_rows = pl.ds(pl.multiple_of(x * rows, rows), rows)
    mine = pl.ds(pl.multiple_of(f * part, part), part)

    def window_copy(j, other):
        return remote(
            tsend.at[j, other], trecv.at[f, j], t_send.at[other, j], t_recv.at[f, j], frame=other
        )

    def space_copy(j, other):
        return remote(
            kv.at[j, :, my_rows], kv.at[j, :, my_rows], s_send.at[other, j], s_recv.at[x, j], space=other
        )

    def gather(j, _):
        core_copy(j).wait_recv()
        borrowed = share + j < main_count
        for n in range(3):
            head_main = mine_first[j, n]
            head_rest = jnp.where(borrowed, theirs[j, n], mine_first[share + j, n])
            block = jnp.where(main_space == 1, head_rest, head_main)
            for g in range(frames):
                tsend[j, g, n] = block[g * part:(g + 1) * part]
            block = jnp.where(main_space == 1, head_main, head_rest)
            if n < 2:
                kv[j, n, my_rows] = block
            else:
                squery[j] = block
        for other in far_first:
            window_copy(j, other).start()

        @pl.when(j > 0)
        def _():
            for other in others_x:
                space_copy(j - 1, other).start()

        return 0

    lax.fori_loop(0, share, gather, 0)

    def fill_reach(j, _):
        own_slot = j + main_space * share
        far = ((main_space == 1) & (share + j < main_count)).astype(jnp.int32)
        own_reach = jnp.int32(0)
        far_reach = jnp.int32(0)
        for h in range(here):
            own_reach = own_reach + jnp.where(pos[c * here + h] == own_slot, win_ref[c * here + h], 0)
            far_reach = far_reach + jnp.where(
                pos[partner * here + h] == share + j, win_ref[partner * here + h], 0
            )
        tab[j] = far * far_reach + (1 - far) * own_reach
        return 0

    lax.fori_loop(0, share, fill_reach, 0)

    def out_copy(j, other):
        return remote(
            tout.at[j, other], res.at[c * here + share + j, mine], o_send.at[other, j], o_recv.at[f, j], frame=other
        )

    def back_copy(slot, other):
        return remote(
            res.at[c * here + slot], res.at[c * here + slot], r_send.at[other, slot], r_recv.at[c, slot], head=other
        )

    for other in others_x:
        space_copy(share - 1, other).start()

    def step(j, _):
        for other in others_f:
            remote(
                tsend.at[j, other], trecv.at[other, j], t_send.at[other, j], t_recv.at[other, j], frame=other
            ).wait_recv()
        trecv[f, j] = tsend[j, f]
        reach = tab[j]
        qs = [trecv[g, j, 2].astype(jnp.float32) for g in range(frames)]
        ks = [trecv[g, j, 0].astype(jnp.float32) for g in range(frames)]
        vs = [trecv[g, j, 1].astype(jnp.float32) for g in range(frames)]
        for g in range(frames):
            near = [m for m in range(frames) if abs(m - g) <= WMAX]
            scores = []
            for m in near:
                raw = jnp.sum(qs[g] * ks[m], axis=-1, keepdims=True) * scale
                scores.append(jnp.where(reach >= abs(m - g), raw, -1e30))
            peak = functools.reduce(jnp.maximum, scores)
            weights = [jnp.exp(s - peak) for s in scores]
            total = functools.reduce(jnp.add, weights)
            acc = functools.reduce(
                jnp.add,
                [w.astype(jnp.bfloat16).astype(jnp.float32) * vs[m] for w, m in zip(weights, near)],
            )
            tout[j, g] = (acc / total).astype(jnp.bfloat16)
        res[c * here + share + j, mine] = tout[j, f]

        for other in others_x:
            other_rows = pl.ds(pl.multiple_of(other * rows, rows), rows)
            remote(
                kv.at[j, :, other_rows], kv.at[j, :, other_rows],
                s_send.at[other, j], s_recv.at[other, j], space=other,
            ).wait_recv()
        query = squery[j]
        scores = lax.dot_general(
            query, kv[j, 0], (((1,), (1,)), ((), ())), preferred_element_type=jnp.float32
        ) * scale
        peak = jnp.max(scores, axis=1, keepdims=True)
        weights = jnp.exp(scores - peak)
        total = jnp.sum(weights, axis=1, keepdims=True)
        acc = jnp.dot(weights.astype(jnp.bfloat16), kv[j, 1], preferred_element_type=jnp.float32)
        res[c * here + j] = (acc / total).astype(jnp.bfloat16)

        for other in far_first:
            out_copy(j, other).start()

        @pl.when(j > 0)
        def _():
            for other in others_c:
                back_copy(j - 1, other).start()

        return 0

    lax.fori_loop(0, share, step, 0)
    for other in others_c:
        back_copy(share - 1, other).start()

    def forward(j, _):
        for other in others_f:
            theirs = pl.ds(pl.multiple_of(other * part, part), part)
            remote(
                tout.at[j, other], res.at[c * here + share + j, theirs], o_send.at[other, j], o_recv.at[other, j],
                frame=other,
            ).wait_recv()
        for other in others_c:
            back_copy(share + j, other).start()
        return 0

    lax.fori_loop(0, share, forward, 0)

    def arrive(slot, _):
        for other in others_c:
            remote(
                res.at[c * here + slot], res.at[other * here + slot], r_send.at[other, slot], r_recv.at[other, slot], head=other
            ).wait_recv()
        return 0

    lax.fori_loop(0, 2 * share, arrive, 0)

    for i in range(here):
        out_ref[0, :, i * HD:(i + 1) * HD] = res[place[c * here + i]]


    def drain(j, _):
        core_copy(j).wait_send()
        for other in others_f:
            window_copy(j, other).wait_send()
            out_copy(j, other).wait_send()
        for other in others_x:
            space_copy(j, other).wait_send()
        for other in others_c:
            back_copy(j, other).wait_send()
            back_copy(share + j, other).wait_send()
        return 0

    lax.fori_loop(0, share, drain, 0)


def local(sizes, queries, key_states, value_states, profile, window):
    frames, spaces, cores = sizes
    rows = queries.shape[1]
    here = queries.shape[2] // HD
    share = here // 2
    part = rows // frames
    any_space = pl.BlockSpec(memory_space=pl.ANY)
    bf = jnp.bfloat16
    dma = pltpu.SemaphoreType.DMA
    return pl.pallas_call(
        functools.partial(kernel, frames, spaces, cores),
        out_shape=pltpu.VMEM(queries.shape, queries.dtype),
        in_specs=[any_space] * 5,
        out_specs=pl.BlockSpec(memory_space=pltpu.VMEM),
        scratch_shapes=[
            pltpu.VMEM((3, here, rows, HD), bf),
            pltpu.VMEM((here, 3, rows, HD), bf),
            pltpu.VMEM((share, 3, rows, HD), bf),
            pltpu.VMEM((share, rows, HD), bf),
            pltpu.VMEM((share, 2, spaces * rows, HD), bf),
            pltpu.VMEM((share, frames, 3, part, HD), bf),
            pltpu.VMEM((frames, share, 3, part, HD), bf),
            pltpu.VMEM((share, frames, part, HD), bf),
            pltpu.VMEM((cores * 2 * share, rows, HD), bf),
            pltpu.SMEM((here * cores,), jnp.int32),
            pltpu.SMEM((here * cores,), jnp.int32),
            pltpu.SMEM((here * cores,), jnp.int32),
            pltpu.SMEM((here * cores,), jnp.int32),
            pltpu.SMEM((here,), jnp.int32),
            pltpu.SMEM((share,), jnp.int32),
            dma((5,)),
            dma((share,)),
            dma((share,)),
            dma((spaces, share)),
            dma((spaces, share)),
            dma((frames, share)),
            dma((frames, share)),
            dma((frames, share)),
            dma((frames, share)),
            dma((cores, 2 * share)),
            dma((cores, 2 * share)),
        ],
        compiler_params=pltpu.CompilerParams(
            collective_id=0, has_side_effects=True, vmem_limit_bytes=60 * 1024 * 1024
        ),
    )(profile, window, queries, key_states, value_states)


def solution(mesh):
    spec = P(("groups", "frame"), "space", "head")
    sizes = (mesh.shape["frame"], mesh.shape["space"], mesh.shape["head"])
    return jax.shard_map(
        functools.partial(local, sizes),
        mesh=mesh,
        in_specs=(spec, spec, spec, P(), P()),
        out_specs=spec,
        check_vma=False,
    )
```

profile of v0, /device:TPU:0, one launch (start us, length us, event | category | flops | bytes accessed | tf_op | source)
XLA Modules:
  0.0 45.6 jit_solution(10605894521224390058)
XLA Ops:
  0.0 44.7 %shard_map.55 = bf16[1,256,1536]{2,1,0:T(8,128)(2,1)S(1)} custom-call(s32[24]{0:T(128)} %prof_hbm.1, s32[24]{0:T(128)} %win_hbm.1, bf16[1,256,1536]{2,1,0:T(8,128)(2,1)} %q_ref.1, bf16[1,256,1536]{2,1,0:T(8,128)(2,1)} %k_ref.1, bf16[1,256,1536]{2,1,0:T(8,128)(2,1)} %v_ref.1), custom_call_target="tpu_custom_call" | custom-call | tf_op jit(solution)/shard_map/pallas_call | solution.py:299
  44.7 0.9 %copy.7 = bf16[1,256,1536]{2,1,0:T(8,128)(2,1)} copy(bf16[1,256,1536]{2,1,0:T(8,128)(2,1)S(1)} %shard_map.55) | data formatting | bytes 1572864
where the time goes:
time: 45.8 us; the launch traced here: 45.6 us
  Pallas kernels  44.7 us (98%)
  local copies, waits for them, and re-layouts  0.88 us (2%)
    pallas_call x1, Pallas kernels, local(): pl.pallas_call(functools.partial(kernel, frames, spaces, cores), out_shap...  44.7 us

commit v1 on v0

--- a/solution.py
+++ b/solution.py
@@ -1,4 +1,5 @@
 import functools
+import itertools
 
 import jax
 import jax.numpy as jnp
@@ -9,10 +10,12 @@
 
 HD = 128
 WMAX = 4
+CAPS = {0: 2, -1: 2, 1: 2, -2: 1, 2: 1}
+EARLY = 2
 MESH = pl.DeviceIdType.MESH
 
 
-def kernel(
+def shared_kernel(
     frames, spaces, cores, prof_hbm, win_hbm, q_ref, k_ref, v_ref, out_ref,
     full, mine_first, theirs, squery, kv, tsend, trecv, tout, res,
     prof_ref, win_ref, pos, place, order, tab,
@@ -287,19 +290,348 @@
     lax.fori_loop(0, share, drain, 0)
 
 
-def local(sizes, queries, key_states, value_states, profile, window):
+def direct_kernel(
+    frames, spaces, cores, fulls, nears, tab, q_ref, k_ref, v_ref, out_ref,
+    full, kv, tsend, trecv, tout, res, nsend, nrecv,
+    loc_sem, word, s_send, s_recv, t_send, t_recv, o_send, o_recv, n_send, n_recv,
+):
+    rows = q_ref.shape[1]
+    here = q_ref.shape[2] // HD
+    part = rows // frames
+    scale = HD ** (-0.5)
+    f = lax.axis_index("frame")
+    x = lax.axis_index("space")
+    c = lax.axis_index("head")
+    side = f // (frames // 2)
+
+    def each(lower, upper, body):
+        def run(i, _):
+            body(i)
+            return 0
+
+        lax.fori_loop(lower, upper, run, 0)
+
+    def of_core(counts):
+        total = jnp.int32(counts[0])
+        for e in range(1, cores):
+            total = jnp.where(c == e, jnp.int32(counts[e]), total)
+        return total
+
+    n_full = of_core(fulls)
+    n_near = of_core(nears)
+    n_time = n_full + n_near
+    n_space = here - n_time
+
+    def remote(src, dst, send, recv, **target):
+        return pltpu.make_async_remote_copy(
+            src_ref=src, dst_ref=dst, send_sem=send, recv_sem=recv,
+            device_id=target, device_id_type=MESH,
+        )
+
+    def lanes(h):
+        return pl.ds(pl.multiple_of(h * HD, HD), HD)
+
+    def there(way, d):
+        other = f + (2 * way - 1) * d
+        return (other >= 0) & (other < frames)
+
+    def away(way, d):
+        return jnp.clip(f + (2 * way - 1) * d, 0, frames - 1)
+
+    barrier = pltpu.get_barrier_semaphore()
+    for d in range(1, spaces):
+        pl.semaphore_signal(
+            barrier, inc=1, device_id={"space": lax.rem(x + d, spaces)}, device_id_type=MESH
+        )
+    for way in range(2):
+        @pl.when(there(way, 1))
+        def _():
+            pl.semaphore_signal(barrier, inc=1, device_id={"frame": away(way, 1)}, device_id_type=MESH)
+
+    def all_in(view, sem):
+        pltpu.make_async_copy(view, view, sem).wait()
+
+    for n, src in enumerate((k_ref, v_ref, q_ref)):
+        each(0, here, lambda h: pltpu.make_async_copy(
+            src.at[0, :, lanes(h)], full.at[n, h], loc_sem.at[0]).start())
+    all_in(full, loc_sem.at[0])
+
+    pl.semaphore_wait(
+        barrier, spaces - 1 + there(0, 1).astype(jnp.int32) + there(1, 1).astype(jnp.int32)
+    )
+
+    def tell(way, d):
+        @pl.when(there(way, d) & there(1 - way, 1))
+        def _():
+            pl.semaphore_signal(
+                word.at[way, d - 1], inc=1, device_id={"frame": away(1 - way, 1)}, device_id_type=MESH
+            )
+
+    if frames > 2:
+        for way in range(2):
+            tell(way, 1)
+
+    my_rows = pl.ds(pl.multiple_of(x * rows, rows), rows)
+    mine = pl.ds(pl.multiple_of(f * part, part), part)
+
+    def window_copy(j, other):
+        return remote(
+            tsend.at[j, other], trecv.at[f, j], t_send.at[0], t_recv.at[j], frame=other
+        )
+
+    def space_copy(j, other):
+        return remote(
+            kv.at[j, :, my_rows], kv.at[j, :, my_rows], s_send.at[0], s_recv.at[j], space=other
+        )
+
+    def out_copy(j, other):
+        return remote(
+            tout.at[j, other], res.at[j, mine], o_send.at[0], o_recv.at[0], frame=other
+        )
+
+    def near_copy(j, way):
+        return remote(
+            nsend.at[j], nrecv.at[1 - way, j], n_send.at[way], n_recv.at[1 - way], frame=away(way, 1)
+        )
+
+    def other_spaces(body):
+        each(1, spaces, lambda d: body(lax.rem(x + d, spaces)))
+
+    def far_first(body):
+        each(0, frames - 1, lambda i: body(
+            lax.rem(f + (1 - side) * (frames - 1 - i) + side * (1 + i), frames)))
+
+    def head_of(slot):
+        return tab[slot]
+
+    def send_at(j, d):
+        def one(way):
+            @pl.when(there(way, d))
+            def _():
+                window_copy(j, away(way, d)).start()
+
+        each(0, 2, one)
+
+    def prepare_space(j):
+        head = head_of(n_time + j)
+        for n in range(2):
+            kv[j, n, my_rows] = full[n, head]
+        other_spaces(lambda other: space_copy(j, other).start())
+
+    def prepare(j):
+        @pl.when(j < n_full)
+        def _():
+            head = head_of(j)
+            for n in range(3):
+                block = full[n, head]
+                for g in range(frames):
+                    tsend[j, g, n] = block[g * part:(g + 1) * part]
+            send_at(j, 1)
+
+        @pl.when(j == EARLY - 1)
+        def _():
+            each(0, n_space, prepare_space)
+            for d in range(2, frames):
+                for way in range(2):
+                    @pl.when(there(way, d))
+                    def _():
+                        pl.semaphore_wait(word.at[way, d - 2], 1)
+
+                    if d < frames - 1:
+                        tell(way, d)
+
+        @pl.when(j >= EARLY - 1)
+        def _():
+            each(2, frames, lambda i: send_at(j - EARLY + 1, frames + 1 - i))
+
+    each(0, n_full + EARLY - 1, prepare)
+
+    def prepare_near(j):
+        head = head_of(n_full + j)
+        for n in range(2):
+            nsend[j, n] = full[n, head]
+
+        def one(way):
+            @pl.when(there(way, 1))
+            def _():
+                near_copy(j, way).start()
+
+        each(0, 2, one)
+
+    if max(nears) > 0:
+        each(0, n_near, prepare_near)
+
+    fine = min(part, 16)
+    wide = min(rows, 128)
+
+    def weigh(scores, values):
+        peak = functools.reduce(jnp.maximum, scores)
+        weights = [jnp.exp(s - peak) for s in scores]
+        total = functools.reduce(jnp.add, weights)
+        acc = functools.reduce(
+            jnp.add,
+            [w.astype(jnp.bfloat16).astype(jnp.float32) * v for w, v in zip(weights, values)],
+        )
+        return (acc / total).astype(jnp.bfloat16)
+
+    def step(j):
+        @pl.when(j < n_full)
+        def _():
+            all_in(trecv.at[pl.ds(0, frames - 1), j], t_recv.at[j])
+            trecv[f, j] = tsend[j, f]
+            reach = tab[2 * here + j]
+
+            def rows_step(i):
+                at = pl.ds(pl.multiple_of(i * fine, fine), fine)
+                qs = [trecv[g, j, 2, at].astype(jnp.float32) for g in range(frames)]
+                ks = [trecv[g, j, 0, at].astype(jnp.float32) for g in range(frames)]
+                vs = [trecv[g, j, 1, at].astype(jnp.float32) for g in range(frames)]
+                for g in range(frames):
+                    close = [m for m in range(frames) if abs(m - g) <= WMAX]
+                    scores = []
+                    for m in close:
+                        raw = jnp.sum(qs[g] * ks[m], axis=-1, keepdims=True) * scale
+                        scores.append(jnp.where(reach >= abs(m - g), raw, -1e30))
+                    tout[j, g, at] = weigh(scores, [vs[m] for m in close])
+
+            each(0, part // fine, rows_step)
+            res[j, mine] = tout[j, f]
+            far_first(lambda other: out_copy(j, other).start())
+
+        @pl.when(j < n_space)
+        def _():
+            all_in(kv.at[j, :, pl.ds(0, (spaces - 1) * rows)], s_recv.at[j])
+            head = head_of(n_time + j)
+
+            def query_step(i):
+                at = pl.ds(pl.multiple_of(i * wide, wide), wide)
+                scores = lax.dot_general(
+                    full[2, head, at], kv[j, 0], (((1,), (1,)), ((), ())), preferred_element_type=jnp.float32
+                ) * scale
+                peak = jnp.max(scores, axis=1, keepdims=True)
+                weights = jnp.exp(scores - peak)
+                total = jnp.sum(weights, axis=1, keepdims=True)
+                acc = jnp.dot(weights.astype(jnp.bfloat16), kv[j, 1], preferred_element_type=jnp.float32)
+                res[n_time + j, at] = (acc / total).astype(jnp.bfloat16)
+
+            each(0, rows // wide, query_step)
+
+    each(0, here, step)
+
+    def by_core(counts, body):
+        for e in range(cores):
+            if counts[e] > 0:
+                @pl.when(c == e)
+                def _():
+                    body(counts[e])
+
+    def near_arrivals(count):
+        for way in range(2):
+            @pl.when(there(way, 1))
+            def _():
+                all_in(nrecv.at[way, pl.ds(0, count)], n_recv.at[way])
+
+            @pl.when(jnp.logical_not(there(way, 1)))
+            def _():
+                nrecv[way, pl.ds(0, count)] = nsend[pl.ds(0, count)]
+
+    by_core(nears, near_arrivals)
+
+    def near_step(j):
+        head = head_of(n_full + j)
+
+        def rows_step(i):
+            at = pl.ds(pl.multiple_of(i * fine, fine), fine)
+            query = full[2, head, at].astype(jnp.float32)
+            keys = (nrecv[0, j, 0, at], nsend[j, 0, at], nrecv[1, j, 0, at])
+            values = (nrecv[0, j, 1, at], nsend[j, 1, at], nrecv[1, j, 1, at])
+            scores = []
+            for key, take in zip(keys, (there(0, 1), None, there(1, 1))):
+                raw = jnp.sum(query * key.astype(jnp.float32), axis=-1, keepdims=True) * scale
+                scores.append(raw if take is None else jnp.where(take, raw, -1e30))
+            res[n_full + j, at] = weigh(scores, [v.astype(jnp.float32) for v in values])
+
+        each(0, rows // fine, rows_step)
+
+    if max(nears) > 0:
+        each(0, n_near, near_step)
+
+    by_core(fulls, lambda count: all_in(res.at[pl.ds(0, count), pl.ds(0, rows - part)], o_recv.at[0]))
+
+    def place(i):
+        out_ref[0, :, lanes(i)] = res[tab[here + i]]
+
+    each(0, here, place)
+
+    def near_sent(count):
+        for way in range(2):
+            @pl.when(there(way, 1))
+            def _():
+                all_in(nsend.at[pl.ds(0, count)], n_send.at[way])
+
+    by_core(fulls, lambda count: all_in(tsend.at[pl.ds(0, count), pl.ds(0, frames - 1)], t_send.at[0]))
+    by_core(fulls, lambda count: all_in(tout.at[pl.ds(0, count), pl.ds(0, frames - 1)], o_send.at[0]))
+    by_core(
+        [here - t - n for t, n in zip(fulls, nears)],
+        lambda count: [all_in(kv.at[pl.ds(0, count), :, pl.ds(0, rows)], s_send.at[0]) for _ in range(1, spaces)],
+    )
+    by_core(nears, near_sent)
+
+
+def direct(sizes, times, nears, number, queries, key_states, value_states, profile, window, table):
+    frames, spaces, cores = sizes
+    rows = queries.shape[1]
+    here = queries.shape[2] // HD
+    part = rows // frames
+    fulls = tuple(t - n for t, n in zip(times, nears))
+    most_full, most_near = max(1, *fulls), max(1, *nears)
+    most_space = max(1, *(here - t for t in times))
+    bf = jnp.bfloat16
+    dma = pltpu.SemaphoreType.DMA
+    return pl.pallas_call(
+        functools.partial(direct_kernel, frames, spaces, cores, fulls, nears),
+        out_shape=pltpu.VMEM(queries.shape, queries.dtype),
+        in_specs=[pl.BlockSpec(memory_space=pltpu.SMEM)] + [pl.BlockSpec(memory_space=pltpu.HBM)] * 3,
+        out_specs=pl.BlockSpec(memory_space=pltpu.VMEM),
+        scratch_shapes=[
+            pltpu.VMEM((3, here, rows, HD), bf),
+            pltpu.VMEM((most_space, 2, spaces * rows, HD), bf),
+            pltpu.VMEM((most_full, frames, 3, part, HD), bf),
+            pltpu.VMEM((frames, most_full, 3, part, HD), bf),
+            pltpu.VMEM((most_full, frames, part, HD), bf),
+            pltpu.VMEM((here, rows, HD), bf),
+            pltpu.VMEM((most_near, 2, rows, HD), bf),
+            pltpu.VMEM((2, most_near, 2, rows, HD), bf),
+            dma((1,)),
+            pltpu.SemaphoreType.REGULAR((2, max(1, frames - 2))),
+            dma((1,)),
+            dma((most_space,)),
+            dma((1,)),
+            dma((most_full,)),
+            dma((1,)),
+            dma((1,)),
+            dma((2,)),
+            dma((2,)),
+        ],
+        compiler_params=pltpu.CompilerParams(
+            collective_id=number, has_side_effects=True, vmem_limit_bytes=60 * 1024 * 1024
+        ),
+    )(table, queries, key_states, value_states)
+
+
+def shared(sizes, queries, key_states, value_states, profile, window, table):
     frames, spaces, cores = sizes
     rows = queries.shape[1]
     here = queries.shape[2] // HD
     share = here // 2
     part = rows // frames
-    any_space = pl.BlockSpec(memory_space=pl.ANY)
+    any_space = pl.BlockSpec(memory_space=pltpu.HBM)
     bf = jnp.bfloat16
     dma = pltpu.SemaphoreType.DMA
     return pl.pallas_call(
-        functools.partial(kernel, frames, spaces, cores),
+        functools.partial(shared_kernel, frames, spaces, cores),
         out_shape=pltpu.VMEM(queries.shape, queries.dtype),
-        in_specs=[any_space] * 5,
+        in_specs=[pl.BlockSpec(memory_space=pltpu.VMEM)] * 2 + [any_space] * 3,
         out_specs=pl.BlockSpec(memory_space=pltpu.VMEM),
         scratch_shapes=[
             pltpu.VMEM((3, here, rows, HD), bf),
@@ -335,6 +667,83 @@
     )(profile, window, queries, key_states, value_states)
 
 
+def choose_kernel(
+    cores, caps, prof_ref, win_ref, prof_hbm, win_hbm, out_ref, tab, prof_out, win_out, sem
+):
+    here = prof_ref.shape[0] // cores
+    c = lax.axis_index("head")
+    copies = (
+        pltpu.make_async_copy(prof_hbm, prof_out, sem.at[0]),
+        pltpu.make_async_copy(win_hbm, win_out, sem.at[1]),
+    )
+    for copy in copies:
+        copy.start()
+    first = jnp.int32(0)
+    for h in range(here):
+        first = first + 1 - prof_ref[h]
+    nears = []
+    for e in range(cores):
+        near = jnp.int32(0)
+        for h in range(e * here, (e + 1) * here):
+            near = near + (1 - prof_ref[h]) * (win_ref[h] == 1).astype(jnp.int32)
+        nears.append(near)
+    index = jnp.int32(0)
+    base = 1
+    for count, cap in caps.items():
+        here_index = jnp.int32(0)
+        for near in nears:
+            here_index = here_index * (cap + 1) + jnp.minimum(near, cap)
+        index = jnp.where(first == count, base + here_index, index)
+        base = base + (cap + 1) ** cores
+    out_ref[0] = index
+
+    kinds = []
+    for h in range(here):
+        p = prof_ref[c * here + h]
+        kinds.append(p * 2 + (1 - p) * (win_ref[c * here + h] == 1).astype(jnp.int32))
+    tops = [jnp.int32(0)]
+    for kind in range(2):
+        top = tops[-1]
+        for h in range(here):
+            top = top + (kinds[h] == kind).astype(jnp.int32)
+        tops.append(top)
+    for h in range(here):
+        slot = jnp.where(kinds[h] == 0, tops[0], jnp.where(kinds[h] == 1, tops[1], tops[2]))
+        for kind in range(3):
+            tops[kind] = tops[kind] + (kinds[h] == kind).astype(jnp.int32)
+        tab[slot] = h
+        tab[here + h] = slot
+        tab[2 * here + slot] = win_ref[c * here + h]
+    for copy in copies:
+        copy.wait()
+
+
+def local(sizes, queries, key_states, value_states, profile, window):
+    frames, spaces, cores = sizes
+    here = queries.shape[2] // HD
+    caps = {here // 2 + d: cap for d, cap in CAPS.items()}
+    smem = pl.BlockSpec(memory_space=pltpu.SMEM)
+    vmem = pl.BlockSpec(memory_space=pltpu.VMEM)
+    hbm = pl.BlockSpec(memory_space=pltpu.HBM)
+    index, table, profile, window = pl.pallas_call(
+        functools.partial(choose_kernel, cores, caps),
+        out_shape=(
+            pltpu.SMEM((1,), jnp.int32),
+            pltpu.SMEM((3 * here,), jnp.int32),
+            pltpu.VMEM(profile.shape, profile.dtype),
+            pltpu.VMEM(window.shape, window.dtype),
+        ),
+        in_specs=[smem, smem, hbm, hbm],
+        out_specs=(smem, smem, vmem, vmem),
+        scratch_shapes=[pltpu.SemaphoreType.DMA((2,))],
+    )(profile, window, profile, window)
+    ways = [functools.partial(shared, sizes)]
+    for first, cap in caps.items():
+        for nears in itertools.product(range(cap + 1), repeat=cores):
+            ways.append(functools.partial(direct, sizes, (first, here - first), nears, len(ways)))
+    return lax.switch(index[0], ways, queries, key_states, value_states, profile, window, table)
+
+
 def solution(mesh):
     spec = P(("groups", "frame"), "space", "head")
     sizes = (mesh.shape["frame"], mesh.shape["space"], mesh.shape["head"])

time: 45.8 us -> 41.3 us (0.902); the launches traced: 45.6 us -> 41.9 us
  Pallas kernels: 44.7 us -> 40.8 us
    pallas_call x1 -> x2, Pallas kernels: 44.7 us -> 40.8 us  [the longest x1 39.4 us: direct(): pl.pallas_call(functools.partial(direct_kernel, frames, spaces, cores, fu...]
where the time goes in v1:
time: 41.3 us; the launch traced here: 41.9 us
  Pallas kernels  40.8 us (99%)
  local copies, waits for them, and re-layouts  0.88 us (2%)
    pallas_call x1, Pallas kernels, direct(): pl.pallas_call(functools.partial(direct_kernel, frames, spaces, cores, fu...  39.4 us
    pallas_call x1, Pallas kernels, local(): pl.pallas_call(functools.partial(choose_kernel, cores, caps), out_shape=(...  1.36 us
    unnamed x1, local copies, waits for them, and re-layouts  0.88 us

profile of v1, /device:TPU:0, one launch (start us, length us, event | category | flops | bytes accessed | tf_op | source)
XLA Modules:
  0.0 41.9 jit_solution(10667618194122005674)
XLA Ops:
  0.0 1.4 %shard_map.91 = (s32[1]{0:T(128)S(4)}, s32[36]{0:T(128)S(4)}, s32[24]{0:T(128)S(1)}, s32[24]{0:T(128)S(1)}) custom-call(s32[24]{0:T(128)} %prof_hbm.1, s32[24]{0:T(128)} %win_hbm.1, s32[24]{0:T(128)} %prof_hbm.1, s32[24]{0:T(128)} %win_hbm.1), custom_call_target="tpu_custom_call" | custom-call | tf_op jit(solution)/shard_map/pallas_call | solution.py:728
  1.4 39.7 %conditional.1 = (bf16[1,256,1536]{2,1,0:T(8,128)(2,1)S(1)}) conditional(s32[]{:T(128)} %bitcast, (s32[24]{0:T(128)S(1)}, s32[24]{0:T(128)S(1)}, bf16[1,256,1536]{2,1,0:T(8,128)(2,1)}, bf16[1,256,1536]{2,1,0:T(8,128)(2,1)}, bf16[1,256,1536]{2,1,0:T(8,128)(2,1)}) %tuple.113, (s32[36]{0:T(128)S(4)}, ...), branch_computations={%region_0.0_spmd, %region_1.0_spmd, %region_2.0_spmd, %region_3.0_... | conditional | bytes 8 | solution.py:744
  1.6 39.4 %branch_20_fun.1 = bf16[1,256,1536]{2,1,0:T(8,128)(2,1)S(1)} custom-call(s32[36]{0:T(128)S(4)} %get-tuple-element.413.tab, bf16[1,256,1536]{2,1,0:T(8,128)(2,1)} %get-tuple-element.414.q_ref, bf16[1,256,1536]{2,1,0:T(8,128)(2,1)} %get-tuple-element.415.k_ref, bf16[1,256,1536]{2,1,0:T(8,128)(2,1)} %get-tuple-element.416.v_ref), custom_call_target="tpu_custom_call" | custom-call | tf_op jit(solution)/shard_map/cond/branch_20_fun/pallas_call | solution.py:591
  41.0 0.9 %copy.79 = bf16[1,256,1536]{2,1,0:T(8,128)(2,1)} copy(bf16[1,256,1536]{2,1,0:T(8,128)(2,1)S(1)} %get-tuple-element.485) | data formatting | bytes 1572864

commit v2 on v1

--- a/solution.py
+++ b/solution.py
@@ -10,7 +10,7 @@
 
 HD = 128
 WMAX = 4
-CAPS = {0: 2, -1: 2, 1: 2, -2: 1, 2: 1}
+CAPS = {0: (2, 2), -1: (2, 2), 1: (2, 2), -2: (1, 2), 2: (0, 1)}
 EARLY = 2
 MESH = pl.DeviceIdType.MESH
 
@@ -272,7 +272,7 @@
     lax.fori_loop(0, 2 * share, arrive, 0)
 
     for i in range(here):
-        out_ref[0, :, i * HD:(i + 1) * HD] = res[place[c * here + i]]
+        out_ref[i] = res[place[c * here + i]]
 
 
     def drain(j, _):
@@ -291,8 +291,8 @@
 
 
 def direct_kernel(
-    frames, spaces, cores, fulls, nears, tab, q_ref, k_ref, v_ref, out_ref,
-    full, kv, tsend, trecv, tout, res, nsend, nrecv,
+    frames, spaces, cores, fulls, nears, tab, q_ref, k_ref, v_ref, res,
+    full, kv, tsend, trecv, tout, nsend, nrecv,
     loc_sem, word, s_send, s_recv, t_send, t_recv, o_send, o_recv, n_send, n_recv,
 ):
     rows = q_ref.shape[1]
@@ -558,10 +558,6 @@
 
     by_core(fulls, lambda count: all_in(res.at[pl.ds(0, count), pl.ds(0, rows - part)], o_recv.at[0]))
 
-    def place(i):
-        out_ref[0, :, lanes(i)] = res[tab[here + i]]
-
-    each(0, here, place)
 
     def near_sent(count):
         for way in range(2):
@@ -590,7 +586,7 @@
     dma = pltpu.SemaphoreType.DMA
     return pl.pallas_call(
         functools.partial(direct_kernel, frames, spaces, cores, fulls, nears),
-        out_shape=pltpu.VMEM(queries.shape, queries.dtype),
+        out_shape=pltpu.VMEM((here, rows, HD), queries.dtype),
         in_specs=[pl.BlockSpec(memory_space=pltpu.SMEM)] + [pl.BlockSpec(memory_space=pltpu.HBM)] * 3,
         out_specs=pl.BlockSpec(memory_space=pltpu.VMEM),
         scratch_shapes=[
@@ -599,7 +595,6 @@
             pltpu.VMEM((most_full, frames, 3, part, HD), bf),
             pltpu.VMEM((frames, most_full, 3, part, HD), bf),
             pltpu.VMEM((most_full, frames, part, HD), bf),
-            pltpu.VMEM((here, rows, HD), bf),
             pltpu.VMEM((most_near, 2, rows, HD), bf),
             pltpu.VMEM((2, most_near, 2, rows, HD), bf),
             dma((1,)),
@@ -630,7 +625,7 @@
     dma = pltpu.SemaphoreType.DMA
     return pl.pallas_call(
         functools.partial(shared_kernel, frames, spaces, cores),
-        out_shape=pltpu.VMEM(queries.shape, queries.dtype),
+        out_shape=pltpu.VMEM((here, rows, HD), queries.dtype),
         in_specs=[pl.BlockSpec(memory_space=pltpu.VMEM)] * 2 + [any_space] * 3,
         out_specs=pl.BlockSpec(memory_space=pltpu.VMEM),
         scratch_shapes=[
@@ -667,6 +662,18 @@
     )(profile, window, queries, key_states, value_states)
 
 
+def place_kernel(tab, res, out_ref, sem):
+    here = res.shape[0]
+
+    def put(slot, _):
+        at = pl.ds(pl.multiple_of(tab[slot] * HD, HD), HD)
+        pltpu.make_async_copy(res.at[slot], out_ref.at[0, :, at], sem.at[0]).start()
+        return 0
+
+    lax.fori_loop(0, here, put, 0)
+    pltpu.make_async_copy(res, res, sem.at[0]).wait()
+
+
 def choose_kernel(
     cores, caps, prof_ref, win_ref, prof_hbm, win_hbm, out_ref, tab, prof_out, win_out, sem
 ):
@@ -689,12 +696,14 @@
         nears.append(near)
     index = jnp.int32(0)
     base = 1
-    for count, cap in caps.items():
+    for count, most in caps.items():
         here_index = jnp.int32(0)
-        for near in nears:
+        size = 1
+        for near, cap in zip(nears, most):
             here_index = here_index * (cap + 1) + jnp.minimum(near, cap)
+            size = size * (cap + 1)
         index = jnp.where(first == count, base + here_index, index)
-        base = base + (cap + 1) ** cores
+        base = base + size
     out_ref[0] = index
 
     kinds = []
@@ -714,6 +723,11 @@
         tab[slot] = h
         tab[here + h] = slot
         tab[2 * here + slot] = win_ref[c * here + h]
+    @pl.when(index == 0)
+    def _():
+        for h in range(here):
+            tab[h] = h
+
     for copy in copies:
         copy.wait()
 
@@ -721,7 +735,7 @@
 def local(sizes, queries, key_states, value_states, profile, window):
     frames, spaces, cores = sizes
     here = queries.shape[2] // HD
-    caps = {here // 2 + d: cap for d, cap in CAPS.items()}
+    caps = {here // 2 + d: most for d, most in CAPS.items()}
     smem = pl.BlockSpec(memory_space=pltpu.SMEM)
     vmem = pl.BlockSpec(memory_space=pltpu.VMEM)
     hbm = pl.BlockSpec(memory_space=pltpu.HBM)
@@ -738,10 +752,17 @@
         scratch_shapes=[pltpu.SemaphoreType.DMA((2,))],
     )(profile, window, profile, window)
     ways = [functools.partial(shared, sizes)]
-    for first, cap in caps.items():
-        for nears in itertools.product(range(cap + 1), repeat=cores):
+    for first, most in caps.items():
+        for nears in itertools.product(*(range(cap + 1) for cap in most)):
             ways.append(functools.partial(direct, sizes, (first, here - first), nears, len(ways)))
-    return lax.switch(index[0], ways, queries, key_states, value_states, profile, window, table)
+    result = lax.switch(index[0], ways, queries, key_states, value_states, profile, window, table)
+    return pl.pallas_call(
+        place_kernel,
+        out_shape=jax.ShapeDtypeStruct(queries.shape, queries.dtype),
+        in_specs=[smem, vmem],
+        out_specs=hbm,
+        scratch_shapes=[pltpu.SemaphoreType.DMA((1,))],
+    )(table, result)
 
 
 def solution(mesh):

time: 41.3 us -> 40.5 us (0.981)
  the two profiles are of different devices: /device:TPU:0 before, /device:TPU:1 now
where the time goes in v2:
time: 40.5 us; the launch traced here: 41 us
  Pallas kernels  40.5 us (100%)
    pallas_call x1, Pallas kernels, direct(): pl.pallas_call(functools.partial(direct_kernel, frames, spaces, cores, fu...  38.3 us
    pallas_call x1, Pallas kernels, local(): pl.pallas_call(functools.partial(choose_kernel, cores, caps), out_shape=(...  1.36 us
    pallas_call x1, Pallas kernels, local(): pl.pallas_call(place_kernel, out_shape=jax.ShapeDtypeStruct(queries.shape...  0.88 us

profile of v2, /device:TPU:1, one launch (start us, length us, event | category | flops | bytes accessed | tf_op | source)
XLA Modules:
  0.0 41.0 jit_solution(14150560044207174372)
XLA Ops:
  0.0 1.4 %shard_map.55 = (s32[1]{0:T(128)S(4)}, s32[36]{0:T(128)S(4)}, s32[24]{0:T(128)S(1)}, s32[24]{0:T(128)S(1)}) custom-call(s32[24]{0:T(128)} %prof_hbm.1, s32[24]{0:T(128)} %win_hbm.1, s32[24]{0:T(128)} %prof_hbm.1, s32[24]{0:T(128)} %win_hbm.1), custom_call_target="tpu_custom_call" | custom-call | tf_op jit(solution)/shard_map/pallas_call | solution.py:742
  1.4 38.6 %conditional.1 = (bf16[12,256,128]{2,1,0:T(8,128)(2,1)S(1)}) conditional(s32[]{:T(128)} %bitcast, (s32[24]{0:T(128)S(1)}, s32[24]{0:T(128)S(1)}, bf16[1,256,1536]{2,1,0:T(8,128)(2,1)}, bf16[1,256,1536]{2,1,0:T(8,128)(2,1)}, bf16[1,256,1536]{2,1,0:T(8,128)(2,1)}) %tuple.113, (s32[36]{0:T(128)S(4)}, ...), branch_computations={%region_0.0_spmd, %region_1.0_spmd, %region_2.0_spmd, %region_3.0_... | conditional | bytes 8 | solution.py:758
  1.4 38.3 %branch_13_fun.1 = bf16[12,256,128]{2,1,0:T(8,128)(2,1)S(1)} custom-call(s32[36]{0:T(128)S(4)} %get-tuple-element.385.tab, bf16[1,256,1536]{2,1,0:T(8,128)(2,1)} %get-tuple-element.386.q_ref, bf16[1,256,1536]{2,1,0:T(8,128)(2,1)} %get-tuple-element.387.k_ref, bf16[1,256,1536]{2,1,0:T(8,128)(2,1)} %get-tuple-element.388.v_ref), custom_call_target="tpu_custom_call" | custom-call | tf_op jit(solution)/shard_map/cond/branch_13_fun/pallas_call | solution.py:587
  39.9 0.9 %shard_map.56 = bf16[1,256,1536]{2,1,0:T(8,128)(2,1)} custom-call(s32[36]{0:T(128)S(4)} %get-tuple-element.481.tab, bf16[12,256,128]{2,1,0:T(8,128)(2,1)S(1)} %get-tuple-element.485.res), custom_call_target="tpu_custom_call" | custom-call | tf_op jit(solution)/shard_map/pallas_call | solution.py:759

commit v3 on v2

--- a/solution.py
+++ b/solution.py
@@ -16,9 +16,9 @@
 
 
 def shared_kernel(
-    frames, spaces, cores, prof_hbm, win_hbm, q_ref, k_ref, v_ref, out_ref,
+    frames, spaces, cores, prof_ref, win_ref, q_ref, k_ref, v_ref, out_ref,
     full, mine_first, theirs, squery, kv, tsend, trecv, tout, res,
-    prof_ref, win_ref, pos, place, order, tab,
+    pos, place, order, tab,
     loc_sem, d_send, d_recv, s_send, s_recv, t_send, t_recv, o_send, o_recv, r_send, r_recv,
 ):
     rows = q_ref.shape[1]
@@ -47,12 +47,6 @@
     def lanes(h):
         return pl.ds(pl.multiple_of(h * HD, HD), HD)
 
-    small = (
-        pltpu.make_async_copy(prof_hbm, prof_ref, loc_sem.at[3]),
-        pltpu.make_async_copy(win_hbm, win_ref, loc_sem.at[4]),
-    )
-    for copy in small:
-        copy.start()
     sources = (k_ref, v_ref, q_ref)
     for n, src in enumerate(sources):
         def local_start(h, _):
@@ -68,9 +62,6 @@
         pl.semaphore_signal(barrier, inc=1, device_id={"space": other}, device_id_type=MESH)
     for other in others_f:
         pl.semaphore_signal(barrier, inc=1, device_id={"frame": other}, device_id_type=MESH)
-
-    for copy in small:
-        copy.wait()
 
     count = jnp.int32(0)
     for h in range(here):
@@ -626,7 +617,7 @@
     return pl.pallas_call(
         functools.partial(shared_kernel, frames, spaces, cores),
         out_shape=pltpu.VMEM((here, rows, HD), queries.dtype),
-        in_specs=[pl.BlockSpec(memory_space=pltpu.VMEM)] * 2 + [any_space] * 3,
+        in_specs=[pl.BlockSpec(memory_space=pltpu.SMEM)] * 2 + [any_space] * 3,
         out_specs=pl.BlockSpec(memory_space=pltpu.VMEM),
         scratch_shapes=[
             pltpu.VMEM((3, here, rows, HD), bf),
@@ -638,8 +629,6 @@
             pltpu.VMEM((frames, share, 3, part, HD), bf),
             pltpu.VMEM((share, frames, part, HD), bf),
             pltpu.VMEM((cores * 2 * share, rows, HD), bf),
-            pltpu.SMEM((here * cores,), jnp.int32),
-            pltpu.SMEM((here * cores,), jnp.int32),
             pltpu.SMEM((here * cores,), jnp.int32),
             pltpu.SMEM((here * cores,), jnp.int32),
             pltpu.SMEM((here,), jnp.int32),
@@ -675,16 +664,10 @@
 
 
 def choose_kernel(
-    cores, caps, prof_ref, win_ref, prof_hbm, win_hbm, out_ref, tab, prof_out, win_out, sem
+    cores, caps, prof_ref, win_ref, out_ref, tab, prof_out, win_out
 ):
     here = prof_ref.shape[0] // cores
     c = lax.axis_index("head")
-    copies = (
-        pltpu.make_async_copy(prof_hbm, prof_out, sem.at[0]),
-        pltpu.make_async_copy(win_hbm, win_out, sem.at[1]),
-    )
-    for copy in copies:
-        copy.start()
     first = jnp.int32(0)
     for h in range(here):
         first = first + 1 - prof_ref[h]
@@ -728,8 +711,12 @@
         for h in range(here):
             tab[h] = h
 
-    for copy in copies:
-        copy.wait()
+        def keep(h, _):
+            prof_out[h] = prof_ref[h]
+            win_out[h] = win_ref[h]
+            return 0
+
+        lax.fori_loop(0, here * cores, keep, 0)
 
 
 def local(sizes, queries, key_states, value_states, profile, window):
@@ -744,13 +731,12 @@
         out_shape=(
             pltpu.SMEM((1,), jnp.int32),
             pltpu.SMEM((3 * here,), jnp.int32),
-            pltpu.VMEM(profile.shape, profile.dtype),
-            pltpu.VMEM(window.shape, window.dtype),
+            pltpu.SMEM(profile.shape, profile.dtype),
+            pltpu.SMEM(window.shape, window.dtype),
         ),
-        in_specs=[smem, smem, hbm, hbm],
-        out_specs=(smem, smem, vmem, vmem),
-        scratch_shapes=[pltpu.SemaphoreType.DMA((2,))],
-    )(profile, window, profile, window)
+        in_specs=[smem, smem],
+        out_specs=(smem, smem, smem, smem),
+    )(profile, window)
     ways = [functools.partial(shared, sizes)]
     for first, most in caps.items():
         for nears in itertools.product(*(range(cap + 1) for cap in most)):

time: 40.5 us -> 40 us (0.988)
  the two profiles are of different devices: /device:TPU:1 before, /device:TPU:0 now
where the time goes in v3:
time: 40 us; the launch traced here: 39.9 us
  Pallas kernels  39.5 us (99%)
    pallas_call x1, Pallas kernels, direct(): pl.pallas_call(functools.partial(direct_kernel, frames, spaces, cores, fu...  37.8 us
    pallas_call x1, Pallas kernels, local(): pl.pallas_call(place_kernel, out_shape=jax.ShapeDtypeStruct(queries.shape...  0.88 us
    pallas_call x1, Pallas kernels, local(): pl.pallas_call(functools.partial(choose_kernel, cores, caps), out_shape=(...  0.86 us

profile of v3, /device:TPU:0, one launch (start us, length us, event | category | flops | bytes accessed | tf_op | source)
XLA Modules:
  0.0 39.9 jit_solution(7603241454685731790)
XLA Ops:
  0.0 0.9 %shard_map.55 = (s32[1]{0:T(128)S(4)}, s32[36]{0:T(128)S(4)}, s32[24]{0:T(128)S(4)}, s32[24]{0:T(128)S(4)}) custom-call(s32[24]{0:T(128)} %prof_ref.1, s32[24]{0:T(128)} %win_ref.1), custom_call_target="tpu_custom_call" | custom-call | tf_op jit(solution)/shard_map/pallas_call | solution.py:729
  0.9 38.0 %conditional.1 = (bf16[12,256,128]{2,1,0:T(8,128)(2,1)S(1)}) conditional(s32[]{:T(128)} %bitcast, (s32[24]{0:T(128)S(4)}, s32[24]{0:T(128)S(4)}, bf16[1,256,1536]{2,1,0:T(8,128)(2,1)}, bf16[1,256,1536]{2,1,0:T(8,128)(2,1)}, bf16[1,256,1536]{2,1,0:T(8,128)(2,1)}) %tuple.113, (s32[36]{0:T(128)S(4)}, ...), branch_computations={%region_0.0_spmd, %region_1.0_spmd, %region_2.0_spmd, %region_3.0_... | conditional | bytes 8 | solution.py:744
  1.1 37.8 %branch_21_fun.1 = bf16[12,256,128]{2,1,0:T(8,128)(2,1)S(1)} custom-call(s32[36]{0:T(128)S(4)} %get-tuple-element.417.tab, bf16[1,256,1536]{2,1,0:T(8,128)(2,1)} %get-tuple-element.418.q_ref, bf16[1,256,1536]{2,1,0:T(8,128)(2,1)} %get-tuple-element.419.k_ref, bf16[1,256,1536]{2,1,0:T(8,128)(2,1)} %get-tuple-element.420.v_ref), custom_call_target="tpu_custom_call" | custom-call | tf_op jit(solution)/shard_map/cond/branch_21_fun/pallas_call | solution.py:578
  38.9 0.9 %shard_map.56 = bf16[1,256,1536]{2,1,0:T(8,128)(2,1)} custom-call(s32[36]{0:T(128)S(4)} %get-tuple-element.481.tab, bf16[12,256,128]{2,1,0:T(8,128)(2,1)S(1)} %get-tuple-element.485.res), custom_call_target="tpu_custom_call" | custom-call | tf_op jit(solution)/shard_map/pallas_call | solution.py:745
